TPU v7x, 32 devices: a whole 2x2x4 slice. The times are simulated.
32 devices in a mesh: group: 2 (over x), serve: 8 (over z, y), tensor: 2 (over core).
Axes of the slice: x: 2, y: 2, z: 4, core: 2. Of those that a mesh axis runs over, the one named last changes fastest.
Arguments:
- tokens: bfloat16 [2048, 8192], P(('group', 'serve'), 'tensor'), parts along dimension 0, may hold values from -70 to 70
- query_weight: bfloat16 [8192, 512], P(None, 'tensor'), may hold values from -0.0625 to 0.0625
- key_value_weight: bfloat16 [8192, 256], P(None, 'tensor'), may hold values from -0.0625 to 0.0625
- output_weight: bfloat16 [512, 8192], P('tensor'), may hold values from -0.25 to 0.25
- adapter_down_maps: bfloat16 [32, 48, 8192], P(('group', 'serve'), None, 'tensor'), parts along dimension 0, may hold values from -0.0625 to 0.0625
- adapter_query_up: bfloat16 [32, 16, 512], P(('group', 'serve'), None, 'tensor'), parts along dimension 0, may hold values from -1.5 to 1.5
- adapter_key_value_up: bfloat16 [32, 16, 256], P(('group', 'serve'), None, 'tensor'), parts along dimension 0, may hold values from -1.5 to 1.5
- adapter_output_down: bfloat16 [32, 16, 512], P(('group', 'serve'), None, 'tensor'), parts along dimension 0, may hold values from -0.25 to 0.25
- adapter_output_up: bfloat16 [32, 16, 8192], P(('group', 'serve'), None, 'tensor'), parts along dimension 0, may hold values from -1.5 to 1.5
- request_adapter: int32 [16], P('group'), parts along dimension 0, may hold values from 0 to 15, as said below
- adapter_pool_row: int32 [32], P('group'), parts along dimension 0, may hold values from 0 to 15, as said below
- lengths: int32 [16], P(('group', 'serve')), parts along dimension 0, may hold values from 16 to 128
Outputs:
- attention_out: bfloat16 [2048, 8192], P(('group', 'serve'), 'tensor'), parts along dimension 0
There are 2 independent parts, one for each index of `group`. A program takes and returns all parts, laid end to end along the dimension named above; an argument that names none is the same for every part. Nothing has to cross between parts.
Inputs may be any that keep to these rules, and one draw needn't show every extreme that they name: Grouping requests by adapter_pool_row[request_adapter[r]] // 2, no group holds more than 4 requests, and some group holds exactly 4. `adapter_pool_row`: each value appears once.
All inputs are finite; a program needn't handle non-finite values.
Results may differ from a plain program's by a relative error of at most 0.012.
The roundings to bfloat16 on the way count: a program that leaves them out, or rounds other values in their place, can miss the bound.
Values may be sent and summed in bfloat16 or wider, within the bound.
A program may use at most 128 MiB of HBM per device.

v0:
```python
import functools

import jax
import jax.numpy as jnp
import numpy as np
from jax import lax
from jax.experimental import pallas as pl
from jax.experimental.pallas import tpu as pltpu
from jax.sharding import PartitionSpec as P

HEAD_SIZE = 128
DOWN_PIECES = 8
UP_PIECES = 2
AHEAD = 2
MESH = pl.DeviceIdType.MESH


def bits_of(size):
    bits = []
    while 2 ** len(bits) < size:
        bits.append(2 ** len(bits))
    return bits[1::-1] + bits[2:]


def subsets(bits):
    masks = [0]
    for bit in bits:
        masks = masks + [mask | bit for mask in masks]
    return masks


def rotary_tables(rows, width):
    half = width // 2
    freqs = np.float32(500000.0) ** (-(np.arange(half, dtype=np.float32) * np.float32(2.0) / np.float32(width)))
    angles = np.arange(rows, dtype=np.float32)[:, None] * freqs.astype(np.float32)[None, :]
    cosine, sine = np.cos(angles), np.sin(angles)
    return np.stack(
        [np.concatenate([cosine, cosine], 1), np.concatenate([-sine, sine], 1)]
    ).astype(np.float32)


def bit_set(number, bit):
    return lax.rem(lax.div(number, bit), 2) == 1


def flip(number, bit):
    return number + bit * (1 - 2 * lax.rem(lax.div(number, bit), 2))


def flip_all(number, mask):
    bit = 1
    while bit <= mask:
        if mask & bit:
            number = flip(number, bit)
        bit *= 2
    return number


def kernel(plan, *refs):
    names = plan["names"]
    r = dict(zip(names, refs))
    size, count, rank = plan["size"], plan["count"], plan["rank"]
    width, q_here, kv_here = plan["width"], plan["q_here"], plan["kv_here"]
    bits, pieces = plan["bits"], plan["pieces"]
    depth = len(bits)
    group = lax.axis_index("group")
    me = lax.axis_index("serve")
    side = lax.axis_index("tensor")
    partner = (group, me, 1 - side)
    neighbours = [(group, flip(me, bit), side) for bit in bits]

    def load(index, src, dst):
        return pltpu.make_async_copy(src, dst, r["load_sem"].at[index])

    own_q = pl.ds(pl.multiple_of(side * q_here, q_here), q_here)
    own_kv = pl.ds(pl.multiple_of(side * kv_here, kv_here), kv_here)
    own_cols = pl.ds(pl.multiple_of(side * width, width), width)
    other_cols = pl.ds(pl.multiple_of((1 - side) * width, width), width)
    loads = [
        load(0, r["adm"], r["down_own"]),
        load(1, r["aqu"], r["small_own"].at[:, :, :q_here]),
        load(2, r["akv"], r["small_own"].at[:, :, q_here : q_here + kv_here]),
        load(3, r["aod"], r["small_own"].at[:, :, q_here + kv_here :]),
        load(4, r["aou"], r["up_own"]),
        load(5, r["tokens"], r["x"].at[side]),
        load(6, r["qw"], r["wq"].at[:, own_q]),
        load(7, r["kvw"], r["wkv"].at[:, own_kv]),
        load(8, r["ow"].at[:, own_cols], r["wo"].at[side]),
        load(9, r["rope"], r["rope_v"]),
    ]
    for copy in loads:
        copy.start()

    barrier = pltpu.get_barrier_semaphore()
    for device in neighbours + [partner]:
        pl.semaphore_signal(barrier, inc=1, device_id=device, device_id_type=MESH)
    pl.semaphore_wait(barrier, len(neighbours) + 1)

    def remote(src, dst, send_sem, recv_sem, device):
        return pltpu.make_async_remote_copy(
            src_ref=src, dst_ref=dst, send_sem=send_sem, recv_sem=recv_sem,
            device_id=device, device_id_type=MESH,
        )

    def stage_copy(stage, index):
        family, start, span = pieces[index]
        cols = slice(start, start + span)
        if stage == 0:
            src, dst = r[family + "_own"], r[family + "_near"]
        else:
            src, dst = r[f"{family}_send{stage}"], r[f"{family}_recv{stage}"]
        return remote(
            src.at[:, :, cols], dst.at[:, :, cols],
            r["hop_send"].at[stage, index], r["hop_recv"].at[stage, index],
            neighbours[stage],
        )

    pair = lambda index, src, dst: remote(
        src, dst, r["pair_send"].at[index], r["pair_recv"].at[index], partner
    )
    pair_tokens = pair(0, r["tokens"], r["x"].at[side])
    pair_q = pair(1, r["qw"], r["wq"].at[:, own_q])
    pair_kv = pair(2, r["kvw"], r["wkv"].at[:, own_kv])
    pair_wo = pair(3, r["ow"].at[:, other_cols], r["wo"].at[side])
    pair_small = pair(4, r["small_all"].at[side], r["small_all"].at[side])
    pair_shrink = pair(5, r["shrink_own"], r["shrink_other"])

    facts = {}
    for mask in subsets(bits):
        wanted = r["pool"][r["req"][flip_all(me, mask)]]
        owner = lax.div(wanted, count)
        facts[mask] = (
            wanted - owner * count,
            [bit_set(owner, bit) != bit_set(me, bit) for bit in bits],
        )

    def chosen(index, mask, stages):
        family, start, span = pieces[index]
        cols = slice(start, start + span)
        slot, differs = facts[mask]

        def of_slot(ref):
            value = ref[0, :, cols]
            for other in range(1, count):
                value = lax.select(slot == other, ref[other, :, cols], value)
            return value

        value = lax.select(differs[0], of_slot(r[family + "_near"]), of_slot(r[family + "_own"]))
        for stage in range(1, stages):
            block = subsets(bits[stage + 1 :]).index(mask)
            arrived = r[f"{family}_recv{stage}"][block, :, cols]
            value = lax.select(differs[stage], arrived, value)
        return value

    def send_stage(stage, index):
        family, start, span = pieces[index]
        cols = slice(start, start + span)
        stage_copy(stage - 1, index).wait_recv()
        for block, mask in enumerate(subsets(bits[stage + 1 :])):
            r[f"{family}_send{stage}"][block, :, cols] = chosen(index, mask | bits[stage], stage)
        stage_copy(stage, index).start()

    own_loaded = {"down": (0,), "small": (1, 2, 3), "up": (4,)}
    loaded = set()

    def need_own(family):
        for index in own_loaded[family]:
            if index not in loaded:
                loads[index].wait()
                loaded.add(index)

    def start_first(index):
        need_own(pieces[index][0])
        stage_copy(0, index).start()

    for index in range(AHEAD):
        start_first(index)
    for copy in (pair_tokens, pair_kv, pair_q, pair_wo):
        copy.start()

    contract = lambda a, b: lax.dot_general(
        a, b, (((1,), (1,)), ((), ())), preferred_element_type=jnp.float32
    )
    mul = lambda a, b: jnp.dot(a, b, preferred_element_type=jnp.float32)

    r["qacc"][...] = jnp.zeros_like(r["qacc"])
    r["kvacc"][...] = jnp.zeros_like(r["kvacc"])
    r["shrink_own"][...] = jnp.zeros_like(r["shrink_own"])
    r["up_maps"][...] = jnp.zeros_like(r["up_maps"])
    three = 3 * rank

    def base_block(number):
        tile = width // DOWN_PIECES
        for half in range(2):
            cols = pl.ds(pl.multiple_of(number * tile, tile), tile)
            rows = pl.ds(pl.multiple_of(half * width + number * tile, tile), tile)
            x_block = r["x"][half, :, cols]
            r["qacc"][...] += mul(x_block, r["wq"][rows, :])
            r["kvacc"][...] += mul(x_block, r["wkv"][rows, :])

    def finish(index):
        family, start, span = pieces[index]
        cols = slice(start, start + span)
        stage_copy(depth - 1, index).wait_recv()
        value = chosen(index, 0, depth)
        if family == "down":
            r["shrink_own"][:, :three] += contract(r["x"][side, :, cols], value)
        elif family == "small":
            r["small_all"][side] = value
            pair_small.start()
        else:
            r["up_all"][:, cols] = value

    n = len(pieces)
    last_down = max(i for i, p in enumerate(pieces) if p[0] == "down")
    first_base = n - 6
    base_done = 0

    def step(number, stages):
        if number + AHEAD < n:
            start_first(number + AHEAD)
        for stage in stages:
            index = number - (stage - 1)
            if 0 <= index < n:
                if stage < depth:
                    send_stage(stage, index)
                else:
                    finish(index)

    all_stages = range(1, depth + 1)
    x_ready = False
    for number in range(last_down + depth):
        if number == depth - 1:
            loads[5].wait()
        step(number, all_stages)
        if number == first_base:
            for index in (6, 7):
                loads[index].wait()
            for copy in (pair_tokens, pair_kv, pair_q):
                copy.wait_recv()
        if number >= first_base and base_done < DOWN_PIECES:
            upto = min(DOWN_PIECES, base_done + 2)

            @pl.loop(base_done, upto)
            def _(block):
                base_block(block)

            base_done = upto
    pair_shrink.start()

    pair_small.wait_recv()
    for half in range(2):
        small = r["small_all"][half]
        r["up_maps"][:rank, half * q_here : (half + 1) * q_here] = small[:, :q_here]
        at = 2 * q_here + half * kv_here
        r["up_maps"][(half + 1) * rank : (half + 2) * rank, at : at + kv_here] = small[
            :, q_here : q_here + kv_here
        ]
        r["out_down"][:, half * q_here : (half + 1) * q_here] = small[:, q_here + kv_here :]
    loads[8].wait()
    loads[9].wait()
    pair_wo.wait_recv()
    pair_shrink.wait_recv()

    shrink = (r["shrink_own"][:, :three] + r["shrink_other"][:, :three]).astype(jnp.bfloat16)
    added = mul(shrink, r["up_maps"][...])
    rows_here = shrink.shape[0]
    kv = (r["kvacc"][...] + added[:, 2 * q_here :]).astype(jnp.bfloat16)
    cos_part, sin_part = r["rope_v"][0], r["rope_v"][1]

    def rotate(v):
        return (v * cos_part + pltpu.roll(v, HEAD_SIZE // 2, 1) * sin_part).astype(jnp.bfloat16)

    keys = rotate(kv[:, :HEAD_SIZE].astype(jnp.float32))
    values = kv[:, HEAD_SIZE:]
    heads = 2 * q_here // HEAD_SIZE
    length = r["lengths"][0]
    line = lax.broadcasted_iota(jnp.int32, (rows_here, rows_here), 0)
    column = lax.broadcasted_iota(jnp.int32, (rows_here, rows_here), 1)
    allowed = (column <= line) & (column < length)
    for head in range(heads):
        at = slice(head * HEAD_SIZE, (head + 1) * HEAD_SIZE)
        query = rotate(r["qacc"][:, at] + added[:, at])
        scores = contract(query, keys) * HEAD_SIZE ** (-0.5)
        scores = jnp.where(allowed, scores, -1e30)
        highest = jnp.max(scores, axis=1, keepdims=True)
        expo = jnp.exp(scores - highest)
        weights = (expo / jnp.sum(expo, axis=1, keepdims=True)).astype(jnp.bfloat16)
        r["attended"][:, at] = mul(weights, values).astype(jnp.bfloat16)
    for number in range(last_down + depth, n + depth - 1):
        step(number, range(1, depth))
    low = contract(r["attended"][...], r["out_down"][...]).astype(jnp.bfloat16)
    for index in range(last_down + 1, n):
        finish(index)
    valid = lax.broadcasted_iota(jnp.int32, (rows_here, 1), 0) < length
    tile = min(512, width)

    @pl.loop(0, width // tile)
    def _(block):
        cols = pl.ds(pl.multiple_of(block * tile, tile), tile)
        total = mul(low, r["up_all"][:, cols])
        base = jnp.zeros((rows_here, tile), jnp.float32)
        for half in range(2):
            term = mul(r["attended"][:, half * q_here : (half + 1) * q_here], r["wo"][half, :, cols])
            base = base + term.astype(jnp.bfloat16).astype(jnp.float32)
        r["out"][:, cols] = jnp.where(valid, base + total, 0.0).astype(jnp.bfloat16)

    for index in range(n):
        for stage in range(depth):
            stage_copy(stage, index).wait_send()
    for copy in (pair_tokens, pair_q, pair_kv, pair_wo, pair_small, pair_shrink):
        copy.wait_send()


def local(tokens, qw, kvw, ow, adm, aqu, akv, aod, aou, req, pool, lengths):
    size = lax.axis_size("serve")
    count, rank, out_width = aou.shape
    rows, width = tokens.shape
    q_here, kv_here = qw.shape[1], kvw.shape[1]
    bits = bits_of(size)
    small_width = q_here + kv_here + q_here
    down_span, up_span = width // DOWN_PIECES, out_width // UP_PIECES
    pieces = [("down", i * down_span, down_span) for i in range(DOWN_PIECES)]
    pieces.insert(1, ("small", 0, small_width))
    pieces += [("up", i * up_span, up_span) for i in range(UP_PIECES)]
    shapes = {
        "down": (adm.shape[1], width),
        "small": (rank, small_width),
        "up": (rank, out_width),
    }
    bf16, f32 = jnp.bfloat16, jnp.float32
    scratch = {}
    for family, (lines, span) in shapes.items():
        scratch[family + "_own"] = pltpu.VMEM((count, lines, span), bf16)
        scratch[family + "_near"] = pltpu.VMEM((count, lines, span), bf16)
        for stage in range(1, len(bits)):
            blocks = 2 ** (len(bits) - 1 - stage)
            scratch[f"{family}_send{stage}"] = pltpu.VMEM((blocks, lines, span), bf16)
            scratch[f"{family}_recv{stage}"] = pltpu.VMEM((blocks, lines, span), bf16)
    scratch.update(
        small_all=pltpu.VMEM((2, rank, small_width), bf16),
        up_all=pltpu.VMEM((rank, out_width), bf16),
        x=pltpu.VMEM((2, rows, width), bf16),
        wq=pltpu.VMEM((qw.shape[0], 2 * q_here), bf16),
        wkv=pltpu.VMEM((kvw.shape[0], 2 * kv_here), bf16),
        wo=pltpu.VMEM((2, ow.shape[0], out_width), bf16),
        rope_v=pltpu.VMEM((2, rows, HEAD_SIZE), f32),
        qacc=pltpu.VMEM((rows, 2 * q_here), f32),
        kvacc=pltpu.VMEM((rows, 2 * kv_here), f32),
        shrink_own=pltpu.VMEM((rows, 128), f32),
        shrink_other=pltpu.VMEM((rows, 128), f32),
        up_maps=pltpu.VMEM((3 * rank, 2 * q_here + 2 * kv_here), bf16),
        out_down=pltpu.VMEM((rank, 2 * q_here), bf16),
        attended=pltpu.VMEM((rows, 2 * q_here), bf16),
        load_sem=pltpu.SemaphoreType.DMA((10,)),
        hop_send=pltpu.SemaphoreType.DMA((len(bits), len(pieces))),
        hop_recv=pltpu.SemaphoreType.DMA((len(bits), len(pieces))),
        pair_send=pltpu.SemaphoreType.DMA((6,)),
        pair_recv=pltpu.SemaphoreType.DMA((6,)),
    )
    operands = ["req", "pool", "lengths", "tokens", "qw", "kvw", "ow", "adm", "aqu", "akv", "aod", "aou", "rope"]
    plan = dict(
        names=operands + ["out"] + list(scratch),
        size=size, count=count, rank=rank, width=width, q_here=q_here, kv_here=kv_here,
        bits=bits, pieces=pieces,
    )
    rope = jnp.asarray(rotary_tables(rows, HEAD_SIZE))
    smem = pl.BlockSpec(memory_space=pltpu.SMEM)
    hbm = pl.BlockSpec(memory_space=pl.ANY)
    return pl.pallas_call(
        functools.partial(kernel, plan),
        out_shape=jax.ShapeDtypeStruct((rows, out_width), bf16),
        in_specs=[smem] * 3 + [hbm] * 10,
        out_specs=pl.BlockSpec(memory_space=pltpu.VMEM),
        scratch_shapes=list(scratch.values()),
        compiler_params=pltpu.CompilerParams(
            collective_id=0, has_side_effects=True, vmem_limit_bytes=60 * 1024 * 1024
        ),
        name="routed_attention",
    )(req, pool, lengths, tokens, qw, kvw, ow, adm, aqu, akv, aod, aou, rope)


def solution(mesh):
    placed = (
        P(("group", "serve"), "tensor"),
        P(None, "tensor"),
        P(None, "tensor"),
        P("tensor", None),
        P(("group", "serve"), None, "tensor"),
        P(("group", "serve"), None, "tensor"),
        P(("group", "serve"), None, "tensor"),
        P(("group", "serve"), None, "tensor"),
        P(("group", "serve"), None, "tensor"),
        P("group"),
        P("group"),
        P(("group", "serve")),
    )
    return jax.shard_map(
        local,
        mesh=mesh,
        in_specs=placed,
        out_specs=P(("group", "serve"), "tensor"),
        check_vma=False,
    )
```

profile of v0, /device:TPU:1, one launch (start us, length us, event | category | flops | bytes accessed | tf_op | source)
XLA Modules:
  0.0 56.5 jit_solution(2624195405940056187)
XLA Ops:
  0.7 53.5 %routed_attention.1 = bf16[128,4096]{1,0:T(8,128)(2,1)} custom-call(s32[8]{0:T(128)} %refs_0_.1, s32[16]{0:T(128)} %refs_1_.1, s32[1]{0:T(128)S(6)} %copy.15.refs_2_, bf16[128,4096]{1,0:T(8,128)(2,1)} %refs_3_.1, bf16[8192,256]{1,0:T(8,128)(2,1)} %refs_4_.1, bf16[8192,128]{1,0:T(8,128)(2,1)} %refs_5_.1, bf16[256,8192]{1,0:T(8,128)(2,1)} %refs_6_.1, ...), custom_call_target="tpu_custom_call" | custom-call | tf_op jit(solution)/shard_map/routed_attention/pallas_call | solution.py:370
  54.2 2.3 %copy.16 = bf16[128,4096]{1,0:T(8,128)(2,1)} copy(bf16[128,4096]{1,0:T(8,128)(2,1)} %routed_attention.1) | data formatting | bytes 2097152
where the time goes:
time: 57 us; the launch traced here: 56.5 us
  Pallas kernels  53.5 us (94%)
  local copies, waits for them, and re-layouts  2.29 us (4%)
  between operations  0.66 us (1%)
    pallas_call x1, Pallas kernels, local(): pl.pallas_call(functools.partial(kernel, plan), out_shape=jax.ShapeDtypeS...  53.5 us
    unnamed x1, local copies, waits for them, and re-layouts  2.29 us

commit v1 on v0

v1 whole, which is shorter than its diff:
```python
import functools

import jax
import jax.numpy as jnp
import numpy as np
from jax import lax
from jax.experimental import pallas as pl
from jax.experimental.pallas import tpu as pltpu
from jax.sharding import PartitionSpec as P

HEAD_SIZE = 128
DOWN_PIECES = 8
UP_PIECES = 2
BASE_PIECES = 8
AHEAD = 2
LAG_C = 1
LAG_D = 3
LAG_F = 2
MESH = pl.DeviceIdType.MESH


def rotary_tables(rows, width):
    half = width // 2
    freqs = np.float32(500000.0) ** (-(np.arange(half, dtype=np.float32) * np.float32(2.0) / np.float32(width)))
    angles = np.arange(rows, dtype=np.float32)[:, None] * freqs.astype(np.float32)[None, :]
    cosine, sine = np.cos(angles), np.sin(angles)
    return np.stack(
        [np.concatenate([cosine, cosine], 1), np.concatenate([-sine, sine], 1)]
    ).astype(np.float32)


def hub_of(pair, levels):
    return 2 * pair + 1 if 2 * pair + 1 < levels // 2 else 2 * pair


def kernel(plan, *refs):
    r = dict(zip(plan["names"], refs))
    count, rank, levels = plan["count"], plan["rank"], plan["levels"]
    width, q_here, kv_here = plan["width"], plan["q_here"], plan["kv_here"]
    pieces = plan["pieces"]
    n = len(pieces)
    pairs = levels // 2
    group = lax.axis_index("group")
    me = lax.axis_index("serve")
    side = lax.axis_index("tensor")
    level = lax.div(me, 2)
    col = lax.rem(me, 2)
    pair = lax.div(level, 2)
    upper = jnp.where(2 * pair + 1 < pairs, 0, 1)
    is_hub = lax.rem(level, 2) != upper
    is_end = lax.rem(level, 2) == upper
    mate = level + 1 - 2 * lax.rem(level, 2)
    core_mate = (group, me, 1 - side)
    col_mate = (group, level * 2 + 1 - col, side)
    level_mate = (group, mate * 2 + col, side)

    def load(index, src, dst):
        return pltpu.make_async_copy(src, dst, r["load_sem"].at[index])

    own_q = pl.ds(pl.multiple_of(side * q_here, q_here), q_here)
    own_kv = pl.ds(pl.multiple_of(side * kv_here, kv_here), kv_here)
    own_cols = pl.ds(pl.multiple_of(side * width, width), width)
    other_cols = pl.ds(pl.multiple_of((1 - side) * width, width), width)
    loads = [
        load(0, r["tokens"], r["x"].at[side]),
        load(1, r["qw"], r["wq"].at[:, own_q]),
        load(2, r["kvw"], r["wkv"].at[:, own_kv]),
        load(3, r["ow"].at[:, own_cols], r["wo"].at[side]),
        load(4, r["rope"], r["rope_v"]),
    ]
    load_tokens, load_q, load_kv, load_wo, load_rope = loads
    raw = [r[f"raw{index}"] for index in range(n)]
    give = [r[f"give{index}"] for index in range(n)]
    sends = [r[f"sends{index}"] for index in range(n)]
    hubs = [r[f"hubs{index}"] for index in range(n)]
    on = [r[f"on{index}"] for index in range(n)]
    got = [r[f"got{index}"] for index in range(n)]
    spans = [ref.shape[-1] for ref in got]
    piece_loads = []
    for index, (family, number) in enumerate(pieces):
        copies = []
        for slot, half, dst in ((0, col, raw[index].at[pl.ds(0, count)]), (1, 1 - col, give[index])):
            if family == "small":
                lines = pl.ds(pl.multiple_of(half * (rank // 2), rank // 2), rank // 2)
                at = 0
                for part, name in enumerate(("aqu", "akv", "aod")):
                    wide = r[name].shape[-1]
                    sem = len(loads) + 2 * n + 2 * part + slot
                    copies.append(load(sem, r[name].at[:, lines, :], dst.at[:, :, at : at + wide]))
                    at += wide
            else:
                src = r["adm" if family == "down" else "aou"]
                span = spans[index]
                at = pl.ds(pl.multiple_of((2 * number + half) * span, span), span)
                copies.append(load(len(loads) + 2 * index + slot, src.at[:, :, at], dst))
        piece_loads.append(copies)
    for copies in piece_loads:
        for copy in copies:
            copy.start()
    for copy in loads:
        copy.start()

    barrier = pltpu.get_barrier_semaphore()

    def greet(device):
        pl.semaphore_signal(barrier, inc=1, device_id=device, device_id_type=MESH)

    greet(core_mate)
    greet(col_mate)
    for other in range(levels):
        other_hub = other == hub_of(other // 2, levels)

        @pl.when((level != other) if other_hub else ((level != other) & is_hub))
        def _():
            greet((group, other * 2 + col, side))

    pl.semaphore_wait(barrier, jnp.where(is_hub, levels + 1, pairs + 2))

    def remote(src, dst, send_sem, recv_sem, device):
        return pltpu.make_async_remote_copy(
            src_ref=src, dst_ref=dst, send_sem=send_sem, recv_sem=recv_sem,
            device_id=device, device_id_type=MESH,
        )

    def hop(kind, index, src, dst, device):
        return remote(src, dst, r["hop_send"].at[kind, index], r["hop_recv"].at[kind, index], device)

    def raws(index, at):
        return raw[index].at[pl.ds(at * count, count)]

    def copy_a(index):
        return hop(0, index, give[index], raws(index, 1), col_mate)

    def copy_b_own(index):
        return hop(1, index, raws(index, 0), raws(index, 2), level_mate)

    def copy_b_relay(index):
        return hop(2, index, raws(index, 1), raws(index, 3), level_mate)

    def copy_c(index, to, hub_pair):
        return remote(
            sends[index].at[to],
            hubs[index].at[hub_pair],
            r["c_send"].at[index, to],
            r["c_recv"].at[index, hub_pair],
            (group, to * 2 + col, side),
        )

    def copy_d(index):
        family, number = pieces[index]
        dst = {
            "down": lambda: got[index],
            "small": lambda: r["small_all"].at[side, col],
            "up": lambda: r["up_all"].at[number, col],
        }[family]()
        return hop(3, index, on[index], dst, col_mate)

    pair_copy = lambda index, src, dst: remote(
        src, dst, r["pair_send"].at[index], r["pair_recv"].at[index], core_mate
    )
    pair_tokens = pair_copy(0, r["tokens"], r["x"].at[side])
    pair_q = pair_copy(1, r["qw"], r["wq"].at[:, own_q])
    pair_kv = pair_copy(2, r["kvw"], r["wkv"].at[:, own_kv])
    pair_wo = pair_copy(3, r["ow"].at[:, other_cols], r["wo"].at[side])
    pair_small = pair_copy(4, r["small_all"].at[side], r["small_all"].at[side])
    pair_shrink = pair_copy(5, r["shrink_own"], r["shrink_other"])

    def facts(target):
        wanted = r["pool"][r["req"][target]]
        owner = lax.div(wanted, count)
        owner_level = lax.div(owner, 2)
        away = jnp.where(lax.rem(owner_level, 2) == lax.rem(level, 2), 0, 2)
        aside = jnp.where(lax.rem(owner, 2) == col, 0, 1)
        return (away + aside) * count + wanted - owner * count, lax.div(owner_level, 2)

    own_facts = [facts(level * 2 + col), facts(level * 2 + 1 - col)]
    level_facts = [[facts(to * 2 + col), facts(to * 2 + 1 - col)] for to in range(levels)]

    def cols_of(index, half):
        number, span = pieces[index][1], spans[index]
        return pl.ds(pl.multiple_of((2 * number + half) * span, span), span)

    contract = lambda a, b: lax.dot_general(
        a, b, (((1,), (1,)), ((), ())), preferred_element_type=jnp.float32
    )
    mul = lambda a, b: jnp.dot(a, b, preferred_element_type=jnp.float32)
    three = 3 * rank

    def start(index):
        for copy in piece_loads[index]:
            copy.wait()
        copy_a(index).start()

        @pl.when(is_end)
        def _():
            copy_b_own(index).start()

    def relay(index):
        copy_a(index).wait_recv()

        @pl.when(is_end)
        def _():
            copy_b_relay(index).start()

    def choose(index):
        @pl.when(is_hub)
        def _():
            copy_b_own(index).wait_recv()
            copy_b_relay(index).wait_recv()
            for to in sorted(range(levels), key=lambda z: abs(2 * z + 1 - levels)):

                @pl.when(level != to)
                def _():
                    for block in range(2):
                        sends[index][to, block] = raw[index][level_facts[to][block][0]]
                    copy_c(index, to, pair).start()

            for block in range(2):
                hubs[index][pair, block] = raw[index][own_facts[block][0]]

    def pick(index):
        family, number = pieces[index]
        for hub in range(pairs):

            @pl.when(level != hub_of(hub, levels))
            def _():
                copy_c(index, hub_of(hub, levels), hub).wait_recv()

        on[index][...] = hubs[index][own_facts[1][1], 1]
        copy_d(index).start()
        value = hubs[index][own_facts[0][1], 0]
        if family == "down":
            r["shrink_own"][:, :three] += contract(r["x"][side, :, cols_of(index, col)], value)
        elif family == "small":
            r["small_all"][side, col] = value
        else:
            r["up_all"][number, col] = value

    def finish(index):
        family, number = pieces[index]
        copy_d(index).wait_recv()
        if family == "down":
            r["shrink_own"][:, :three] += contract(
                r["x"][side, :, cols_of(index, 1 - col)], got[index][...]
            )
        elif family == "small":
            pair_small.start()

    for index in range(AHEAD):
        start(index)
    for copy in (pair_tokens, pair_kv, pair_q, pair_wo):
        copy.start()

    r["qacc"][...] = jnp.zeros_like(r["qacc"])
    r["kvacc"][...] = jnp.zeros_like(r["kvacc"])
    r["shrink_own"][...] = jnp.zeros_like(r["shrink_own"])
    r["up_maps"][...] = jnp.zeros_like(r["up_maps"])

    def base_block(number):
        tile = width // BASE_PIECES
        for half in range(2):
            cols = pl.ds(pl.multiple_of(number * tile, tile), tile)
            rows = pl.ds(pl.multiple_of(half * width + number * tile, tile), tile)
            x_block = r["x"][half, :, cols]
            r["qacc"][...] += mul(x_block, r["wq"][rows, :])
            r["kvacc"][...] += mul(x_block, r["wkv"][rows, :])

    last_down = max(i for i, p in enumerate(pieces) if p[0] == "down")
    done = {start: AHEAD, relay: 0, choose: 0, pick: 0, finish: 0}
    lags = {start: -AHEAD, relay: 0, choose: LAG_C, pick: LAG_C + LAG_D, finish: LAG_C + LAG_D + LAG_F}

    def up_to(action, index):
        while done[action] <= min(index, n - 1):
            action(done[action])
            done[action] += 1

    base_done = 0
    steps = last_down + lags[finish] + 1
    first_base = steps - 5
    for number in range(steps):
        for action in (start, relay, choose, pick, finish):
            if action is pick and done[pick] == 0 and number == lags[pick]:
                load_tokens.wait()
            up_to(action, number - lags[action])
        if number == first_base:
            load_q.wait()
            load_kv.wait()
            for copy in (pair_tokens, pair_kv, pair_q):
                copy.wait_recv()
        if number >= first_base and base_done < BASE_PIECES:
            upto = min(BASE_PIECES, base_done + 2)

            @pl.loop(base_done, upto)
            def _(block):
                base_block(block)

            base_done = upto
    pair_shrink.start()

    up_to(relay, n)
    up_to(choose, n)
    pair_small.wait_recv()
    lines = rank // 2
    for half in range(2):
        own = slice(half * q_here, (half + 1) * q_here)
        at = 2 * q_here + half * kv_here
        for part in range(2):
            small = r["small_all"][half, part]
            to = slice(part * lines, (part + 1) * lines)
            r["up_maps"][to, own] = small[:, :q_here]
            to_kv = slice((half + 1) * rank + part * lines, (half + 1) * rank + (part + 1) * lines)
            r["up_maps"][to_kv, at : at + kv_here] = small[:, q_here : q_here + kv_here]
            r["out_down"][to, own] = small[:, q_here + kv_here :]
    load_wo.wait()
    load_rope.wait()
    pair_wo.wait_recv()
    pair_shrink.wait_recv()

    shrink = (r["shrink_own"][:, :three] + r["shrink_other"][:, :three]).astype(jnp.bfloat16)
    added = mul(shrink, r["up_maps"][...])
    rows_here = shrink.shape[0]
    kv = (r["kvacc"][...] + added[:, 2 * q_here :]).astype(jnp.bfloat16)
    cos_part, sin_part = r["rope_v"][0], r["rope_v"][1]

    def rotate(v):
        return (v * cos_part + pltpu.roll(v, HEAD_SIZE // 2, 1) * sin_part).astype(jnp.bfloat16)

    keys = rotate(kv[:, :HEAD_SIZE].astype(jnp.float32))
    values = kv[:, HEAD_SIZE:]
    heads = 2 * q_here // HEAD_SIZE
    length = r["lengths"][0]
    line = lax.broadcasted_iota(jnp.int32, (rows_here, rows_here), 0)
    column = lax.broadcasted_iota(jnp.int32, (rows_here, rows_here), 1)
    allowed = (column <= line) & (column < length)
    for head in range(heads):
        at = slice(head * HEAD_SIZE, (head + 1) * HEAD_SIZE)
        query = rotate(r["qacc"][:, at] + added[:, at])
        scores = contract(query, keys) * HEAD_SIZE ** (-0.5)
        scores = jnp.where(allowed, scores, -1e30)
        highest = jnp.max(scores, axis=1, keepdims=True)
        expo = jnp.exp(scores - highest)
        weights = (expo / jnp.sum(expo, axis=1, keepdims=True)).astype(jnp.bfloat16)
        r["attended"][:, at] = mul(weights, values).astype(jnp.bfloat16)
    up_to(pick, n)
    low = contract(r["attended"][...], r["out_down"][...]).astype(jnp.bfloat16)
    up_to(finish, n)
    valid = lax.broadcasted_iota(jnp.int32, (rows_here, 1), 0) < length
    up_span = r["up_all"].shape[-1]
    tile = min(512, up_span)
    per = up_span // tile

    @pl.loop(0, width // tile)
    def _(block):
        cols = pl.ds(pl.multiple_of(block * tile, tile), tile)
        part = lax.div(block, per)
        inner = pl.ds(pl.multiple_of((block - part * per) * tile, tile), tile)
        total = mul(low, r["up_all"][lax.div(part, 2), lax.rem(part, 2), :, inner])
        base = jnp.zeros((rows_here, tile), jnp.float32)
        for half in range(2):
            term = mul(r["attended"][:, half * q_here : (half + 1) * q_here], r["wo"][half, :, cols])
            base = base + term.astype(jnp.bfloat16).astype(jnp.float32)
        r["out"][:, cols] = jnp.where(valid, base + total, 0.0).astype(jnp.bfloat16)

    for index in range(n):
        copy_a(index).wait_send()
        copy_d(index).wait_send()

        @pl.when(is_end)
        def _():
            copy_b_own(index).wait_send()
            copy_b_relay(index).wait_send()

        @pl.when(is_hub)
        def _():
            for to in range(levels):

                @pl.when(level != to)
                def _():
                    copy_c(index, to, pair).wait_send()

    for copy in (pair_tokens, pair_q, pair_kv, pair_wo, pair_small, pair_shrink):
        copy.wait_send()


def local(tokens, qw, kvw, ow, adm, aqu, akv, aod, aou, req, pool, lengths):
    size = lax.axis_size("serve")
    count, rank, out_width = aou.shape
    rows, width = tokens.shape
    q_here, kv_here = qw.shape[1], kvw.shape[1]
    levels = size // 2
    small_width = q_here + kv_here + q_here
    down_span, up_span = width // (2 * DOWN_PIECES), out_width // (2 * UP_PIECES)
    pieces = [("down", i) for i in range(DOWN_PIECES)]
    pieces.insert(1, ("small", 0))
    pieces += [("up", i) for i in range(UP_PIECES)]
    shapes = {
        "down": (adm.shape[1], down_span),
        "small": (rank // 2, small_width),
        "up": (rank, up_span),
    }
    bf16, f32 = jnp.bfloat16, jnp.float32
    scratch = {}
    for index, (family, _) in enumerate(pieces):
        lines, span = shapes[family]
        kinds = {
            "raw": (4 * count,), "give": (count,), "sends": (levels, 2),
            "hubs": (levels // 2, 2), "on": (), "got": (),
        }
        for kind, lead in kinds.items():
            scratch[f"{kind}{index}"] = pltpu.VMEM((*lead, lines, span), bf16)
    scratch.update(
        small_all=pltpu.VMEM((2, 2, rank // 2, small_width), bf16),
        up_all=pltpu.VMEM((UP_PIECES, 2, rank, up_span), bf16),
        x=pltpu.VMEM((2, rows, width), bf16),
        wq=pltpu.VMEM((qw.shape[0], 2 * q_here), bf16),
        wkv=pltpu.VMEM((kvw.shape[0], 2 * kv_here), bf16),
        wo=pltpu.VMEM((2, ow.shape[0], out_width), bf16),
        rope_v=pltpu.VMEM((2, rows, HEAD_SIZE), f32),
        qacc=pltpu.VMEM((rows, 2 * q_here), f32),
        kvacc=pltpu.VMEM((rows, 2 * kv_here), f32),
        shrink_own=pltpu.VMEM((rows, 128), f32),
        shrink_other=pltpu.VMEM((rows, 128), f32),
        up_maps=pltpu.VMEM((3 * rank, 2 * q_here + 2 * kv_here), bf16),
        out_down=pltpu.VMEM((rank, 2 * q_here), bf16),
        attended=pltpu.VMEM((rows, 2 * q_here), bf16),
        load_sem=pltpu.SemaphoreType.DMA((5 + 2 * len(pieces) + 6,)),
        hop_send=pltpu.SemaphoreType.DMA((4, len(pieces))),
        hop_recv=pltpu.SemaphoreType.DMA((4, len(pieces))),
        c_send=pltpu.SemaphoreType.DMA((len(pieces), levels)),
        c_recv=pltpu.SemaphoreType.DMA((len(pieces), levels // 2)),
        pair_send=pltpu.SemaphoreType.DMA((6,)),
        pair_recv=pltpu.SemaphoreType.DMA((6,)),
    )
    operands = ["req", "pool", "lengths", "tokens", "qw", "kvw", "ow", "adm", "aqu", "akv", "aod", "aou", "rope"]
    plan = dict(
        names=operands + ["out"] + list(scratch),
        levels=levels, count=count, rank=rank, width=width, q_here=q_here, kv_here=kv_here,
        pieces=pieces,
    )
    rope = jnp.asarray(rotary_tables(rows, HEAD_SIZE))
    smem = pl.BlockSpec(memory_space=pltpu.SMEM)
    hbm = pl.BlockSpec(memory_space=pl.ANY)
    return pl.pallas_call(
        functools.partial(kernel, plan),
        out_shape=jax.ShapeDtypeStruct((rows, out_width), bf16),
        in_specs=[smem] * 3 + [hbm] * 10,
        out_specs=pl.BlockSpec(memory_space=pltpu.VMEM),
        scratch_shapes=list(scratch.values()),
        compiler_params=pltpu.CompilerParams(
            collective_id=0, has_side_effects=True, vmem_limit_bytes=60 * 1024 * 1024
        ),
        name="routed_attention",
    )(req, pool, lengths, tokens, qw, kvw, ow, adm, aqu, akv, aod, aou, rope)


def solution(mesh):
    placed = (
        P(("group", "serve"), "tensor"),
        P(None, "tensor"),
        P(None, "tensor"),
        P("tensor", None),
        P(("group", "serve"), None, "tensor"),
        P(("group", "serve"), None, "tensor"),
        P(("group", "serve"), None, "tensor"),
        P(("group", "serve"), None, "tensor"),
        P(("group", "serve"), None, "tensor"),
        P("group"),
        P("group"),
        P(("group", "serve")),
    )
    return jax.shard_map(
        local,
        mesh=mesh,
        in_specs=placed,
        out_specs=P(("group", "serve"), "tensor"),
        check_vma=False,
    )
```

time: 57 us -> 48.5 us (0.85)
  Pallas kernels: 53.5 us -> 44.9 us
    pallas_call x1, Pallas kernels: 53.5 us -> 44.9 us  [local(): pl.pallas_call(functools.partial(kernel, plan), out_shape=jax.ShapeDtypeS...]
where the time goes in v1:
time: 48.5 us; the launch traced here: 47.8 us
  Pallas kernels  44.9 us (93%)
  local copies, waits for them, and re-layouts  2.29 us (5%)
  between operations  0.66 us (1%)
    pallas_call x1, Pallas kernels, local(): pl.pallas_call(functools.partial(kernel, plan), out_shape=jax.ShapeDtypeS...  44.9 us
    unnamed x1, local copies, waits for them, and re-layouts  2.29 us

profile of v1, /device:TPU:1, one launch (start us, length us, event | category | flops | bytes accessed | tf_op | source)
XLA Modules:
  0.0 47.8 jit_solution(14682972690597460932)
XLA Ops:
  0.7 44.9 %routed_attention.1 = bf16[128,4096]{1,0:T(8,128)(2,1)} custom-call(s32[8]{0:T(128)} %refs_0_.1, s32[16]{0:T(128)} %refs_1_.1, s32[1]{0:T(128)S(6)} %copy.15.refs_2_, bf16[128,4096]{1,0:T(8,128)(2,1)} %refs_3_.1, bf16[8192,256]{1,0:T(8,128)(2,1)} %refs_4_.1, bf16[8192,128]{1,0:T(8,128)(2,1)} %refs_5_.1, bf16[256,8192]{1,0:T(8,128)(2,1)} %refs_6_.1, ...), custom_call_target="tpu_custom_call" | custom-call | tf_op jit(solution)/shard_map/routed_attention/pallas_call | solution.py:443
  45.5 2.3 %copy.16 = bf16[128,4096]{1,0:T(8,128)(2,1)} copy(bf16[128,4096]{1,0:T(8,128)(2,1)} %routed_attention.1) | data formatting | bytes 2097152

commit v2 on v1

--- a/solution.py
+++ b/solution.py
@@ -14,8 +14,8 @@
 BASE_PIECES = 8
 AHEAD = 2
 LAG_C = 1
-LAG_D = 3
-LAG_F = 2
+LAG_P = 3
+CHOOSE_1 = 9
 MESH = pl.DeviceIdType.MESH
 
 
@@ -73,9 +73,7 @@
     give = [r[f"give{index}"] for index in range(n)]
     sends = [r[f"sends{index}"] for index in range(n)]
     hubs = [r[f"hubs{index}"] for index in range(n)]
-    on = [r[f"on{index}"] for index in range(n)]
-    got = [r[f"got{index}"] for index in range(n)]
-    spans = [ref.shape[-1] for ref in got]
+    spans = [ref.shape[-1] for ref in give]
     piece_loads = []
     for index, (family, number) in enumerate(pieces):
         copies = []
@@ -106,15 +104,18 @@
         pl.semaphore_signal(barrier, inc=1, device_id=device, device_id_type=MESH)
 
     greet(core_mate)
-    greet(col_mate)
-    for other in range(levels):
-        other_hub = other == hub_of(other // 2, levels)
-
-        @pl.when((level != other) if other_hub else ((level != other) & is_hub))
-        def _():
-            greet((group, other * 2 + col, side))
-
-    pl.semaphore_wait(barrier, jnp.where(is_hub, levels + 1, pairs + 2))
+    for other in range(2 * levels):
+        other_hub = other // 2 == hub_of(other // 4, levels)
+
+        @pl.when((me != other) if other_hub else ((me != other) & is_hub))
+        def _():
+            greet((group, other, side))
+
+    @pl.when(is_end)
+    def _():
+        greet(col_mate)
+
+    pl.semaphore_wait(barrier, jnp.where(is_hub, 2 * levels, 2 * pairs + 2))
 
     def remote(src, dst, send_sem, recv_sem, device):
         return pltpu.make_async_remote_copy(
@@ -137,23 +138,14 @@
     def copy_b_relay(index):
         return hop(2, index, raws(index, 1), raws(index, 3), level_mate)
 
-    def copy_c(index, to, hub_pair):
+    def copy_c(index, half, to, hub_pair):
         return remote(
             sends[index].at[to],
-            hubs[index].at[hub_pair],
+            hubs[index].at[half, hub_pair],
             r["c_send"].at[index, to],
-            r["c_recv"].at[index, hub_pair],
-            (group, to * 2 + col, side),
+            r["c_recv"].at[index, half, hub_pair],
+            (group, to, side),
         )
-
-    def copy_d(index):
-        family, number = pieces[index]
-        dst = {
-            "down": lambda: got[index],
-            "small": lambda: r["small_all"].at[side, col],
-            "up": lambda: r["up_all"].at[number, col],
-        }[family]()
-        return hop(3, index, on[index], dst, col_mate)
 
     pair_copy = lambda index, src, dst: remote(
         src, dst, r["pair_send"].at[index], r["pair_recv"].at[index], core_mate
@@ -173,12 +165,8 @@
         aside = jnp.where(lax.rem(owner, 2) == col, 0, 1)
         return (away + aside) * count + wanted - owner * count, lax.div(owner_level, 2)
 
-    own_facts = [facts(level * 2 + col), facts(level * 2 + 1 - col)]
-    level_facts = [[facts(to * 2 + col), facts(to * 2 + 1 - col)] for to in range(levels)]
-
-    def cols_of(index, half):
-        number, span = pieces[index][1], spans[index]
-        return pl.ds(pl.multiple_of((2 * number + half) * span, span), span)
+    mine = facts(me)
+    wants = [facts(to) for to in range(2 * levels)]
 
     contract = lambda a, b: lax.dot_general(
         a, b, (((1,), (1,)), ((), ())), preferred_element_type=jnp.float32
@@ -202,48 +190,42 @@
         def _():
             copy_b_relay(index).start()
 
+    send_order = sorted(range(2 * levels), key=lambda to: -abs(2 * (to // 2) + 1 - levels))
+
     def choose(index):
         @pl.when(is_hub)
         def _():
             copy_b_own(index).wait_recv()
             copy_b_relay(index).wait_recv()
-            for to in sorted(range(levels), key=lambda z: abs(2 * z + 1 - levels)):
-
-                @pl.when(level != to)
+            for to in send_order:
+
+                @pl.when(me != to)
                 def _():
-                    for block in range(2):
-                        sends[index][to, block] = raw[index][level_facts[to][block][0]]
-                    copy_c(index, to, pair).start()
-
-            for block in range(2):
-                hubs[index][pair, block] = raw[index][own_facts[block][0]]
+                    sends[index][to] = raw[index][wants[to][0]]
+                    copy_c(index, col, to, pair).start()
+
+            hubs[index][col, pair] = raw[index][mine[0]]
 
     def pick(index):
         family, number = pieces[index]
-        for hub in range(pairs):
-
-            @pl.when(level != hub_of(hub, levels))
-            def _():
-                copy_c(index, hub_of(hub, levels), hub).wait_recv()
-
-        on[index][...] = hubs[index][own_facts[1][1], 1]
-        copy_d(index).start()
-        value = hubs[index][own_facts[0][1], 0]
-        if family == "down":
-            r["shrink_own"][:, :three] += contract(r["x"][side, :, cols_of(index, col)], value)
-        elif family == "small":
-            r["small_all"][side, col] = value
-        else:
-            r["up_all"][number, col] = value
-
-    def finish(index):
-        family, number = pieces[index]
-        copy_d(index).wait_recv()
-        if family == "down":
-            r["shrink_own"][:, :three] += contract(
-                r["x"][side, :, cols_of(index, 1 - col)], got[index][...]
-            )
-        elif family == "small":
+        for half in range(2):
+            for hub in range(pairs):
+
+                @pl.when(me != 2 * hub_of(hub, levels) + half)
+                def _():
+                    copy_c(index, half, 2 * hub_of(hub, levels) + half, hub).wait_recv()
+
+        for half in range(2):
+            value = hubs[index][half, mine[1]]
+            if family == "down":
+                at = (2 * number + half) * spans[index]
+                x_part = r["x"][side, :, at : at + spans[index]]
+                r["shrink_own"][:, :three] += contract(x_part, value)
+            elif family == "small":
+                r["small_all"][side, half] = value
+            else:
+                r["up_all"][number, half] = value
+        if family == "small":
             pair_small.start()
 
     for index in range(AHEAD):
@@ -266,8 +248,8 @@
             r["kvacc"][...] += mul(x_block, r["wkv"][rows, :])
 
     last_down = max(i for i, p in enumerate(pieces) if p[0] == "down")
-    done = {start: AHEAD, relay: 0, choose: 0, pick: 0, finish: 0}
-    lags = {start: -AHEAD, relay: 0, choose: LAG_C, pick: LAG_C + LAG_D, finish: LAG_C + LAG_D + LAG_F}
+    done = {start: AHEAD, relay: 0, choose: 0, pick: 0}
+    lags = {start: -AHEAD, relay: 0, choose: LAG_C, pick: LAG_C + LAG_P}
 
     def up_to(action, index):
         while done[action] <= min(index, n - 1):
@@ -275,10 +257,10 @@
             done[action] += 1
 
     base_done = 0
-    steps = last_down + lags[finish] + 1
+    steps = last_down + lags[pick] + 1
     first_base = steps - 5
     for number in range(steps):
-        for action in (start, relay, choose, pick, finish):
+        for action in (start, relay, choose, pick):
             if action is pick and done[pick] == 0 and number == lags[pick]:
                 load_tokens.wait()
             up_to(action, number - lags[action])
@@ -298,7 +280,7 @@
     pair_shrink.start()
 
     up_to(relay, n)
-    up_to(choose, n)
+    up_to(choose, CHOOSE_1)
     pair_small.wait_recv()
     lines = rank // 2
     for half in range(2):
@@ -327,6 +309,7 @@
 
     keys = rotate(kv[:, :HEAD_SIZE].astype(jnp.float32))
     values = kv[:, HEAD_SIZE:]
+    up_to(choose, n)
     heads = 2 * q_here // HEAD_SIZE
     length = r["lengths"][0]
     line = lax.broadcasted_iota(jnp.int32, (rows_here, rows_here), 0)
@@ -341,29 +324,31 @@
         expo = jnp.exp(scores - highest)
         weights = (expo / jnp.sum(expo, axis=1, keepdims=True)).astype(jnp.bfloat16)
         r["attended"][:, at] = mul(weights, values).astype(jnp.bfloat16)
-    up_to(pick, n)
     low = contract(r["attended"][...], r["out_down"][...]).astype(jnp.bfloat16)
-    up_to(finish, n)
-    valid = lax.broadcasted_iota(jnp.int32, (rows_here, 1), 0) < length
-    up_span = r["up_all"].shape[-1]
-    tile = min(512, up_span)
-    per = up_span // tile
+    tile = min(512, width)
 
     @pl.loop(0, width // tile)
     def _(block):
         cols = pl.ds(pl.multiple_of(block * tile, tile), tile)
-        part = lax.div(block, per)
-        inner = pl.ds(pl.multiple_of((block - part * per) * tile, tile), tile)
-        total = mul(low, r["up_all"][lax.div(part, 2), lax.rem(part, 2), :, inner])
         base = jnp.zeros((rows_here, tile), jnp.float32)
         for half in range(2):
             term = mul(r["attended"][:, half * q_here : (half + 1) * q_here], r["wo"][half, :, cols])
             base = base + term.astype(jnp.bfloat16).astype(jnp.float32)
-        r["out"][:, cols] = jnp.where(valid, base + total, 0.0).astype(jnp.bfloat16)
+        r["base"][:, cols] = base
+
+    valid = lax.broadcasted_iota(jnp.int32, (rows_here, 1), 0) < length
+    span = r["up_all"].shape[-1]
+    for number in range(UP_PIECES):
+        up_to(pick, last_down + 1 + number)
+
+        for half in range(2):
+            at = (2 * number + half) * span
+            cols = slice(at, at + span)
+            total = r["base"][:, cols] + mul(low, r["up_all"][number, half])
+            r["out"][:, cols] = jnp.where(valid, total, 0.0).astype(jnp.bfloat16)
 
     for index in range(n):
         copy_a(index).wait_send()
-        copy_d(index).wait_send()
 
         @pl.when(is_end)
         def _():
@@ -372,11 +357,11 @@
 
         @pl.when(is_hub)
         def _():
-            for to in range(levels):
-
-                @pl.when(level != to)
+            for to in range(2 * levels):
+
+                @pl.when(me != to)
                 def _():
-                    copy_c(index, to, pair).wait_send()
+                    copy_c(index, col, to, pair).wait_send()
 
     for copy in (pair_tokens, pair_q, pair_kv, pair_wo, pair_small, pair_shrink):
         copy.wait_send()
@@ -391,7 +376,7 @@
     small_width = q_here + kv_here + q_here
     down_span, up_span = width // (2 * DOWN_PIECES), out_width // (2 * UP_PIECES)
     pieces = [("down", i) for i in range(DOWN_PIECES)]
-    pieces.insert(1, ("small", 0))
+    pieces.insert(0, ("small", 0))
     pieces += [("up", i) for i in range(UP_PIECES)]
     shapes = {
         "down": (adm.shape[1], down_span),
@@ -403,8 +388,8 @@
     for index, (family, _) in enumerate(pieces):
         lines, span = shapes[family]
         kinds = {
-            "raw": (4 * count,), "give": (count,), "sends": (levels, 2),
-            "hubs": (levels // 2, 2), "on": (), "got": (),
+            "raw": (4 * count,), "give": (count,), "sends": (size,),
+            "hubs": (2, levels // 2),
         }
         for kind, lead in kinds.items():
             scratch[f"{kind}{index}"] = pltpu.VMEM((*lead, lines, span), bf16)
@@ -424,10 +409,11 @@
         out_down=pltpu.VMEM((rank, 2 * q_here), bf16),
         attended=pltpu.VMEM((rows, 2 * q_here), bf16),
         load_sem=pltpu.SemaphoreType.DMA((5 + 2 * len(pieces) + 6,)),
-        hop_send=pltpu.SemaphoreType.DMA((4, len(pieces))),
-        hop_recv=pltpu.SemaphoreType.DMA((4, len(pieces))),
-        c_send=pltpu.SemaphoreType.DMA((len(pieces), levels)),
-        c_recv=pltpu.SemaphoreType.DMA((len(pieces), levels // 2)),
+        hop_send=pltpu.SemaphoreType.DMA((3, len(pieces))),
+        hop_recv=pltpu.SemaphoreType.DMA((3, len(pieces))),
+        c_send=pltpu.SemaphoreType.DMA((len(pieces), size)),
+        c_recv=pltpu.SemaphoreType.DMA((len(pieces), 2, levels // 2)),
+        base=pltpu.VMEM((rows, out_width), f32),
         pair_send=pltpu.SemaphoreType.DMA((6,)),
         pair_recv=pltpu.SemaphoreType.DMA((6,)),
     )

time: 48.5 us -> 44.6 us (0.920); the launches traced: 47.8 us -> 44.5 us
  Pallas kernels: 44.9 us -> 41.5 us
    pallas_call x1, Pallas kernels: 44.9 us -> 41.5 us  [local(): pl.pallas_call(functools.partial(kernel, plan), out_shape=jax.ShapeDtypeS...]
where the time goes in v2:
time: 44.6 us; the launch traced here: 44.5 us
  Pallas kernels  41.5 us (93%)
  local copies, waits for them, and re-layouts  2.29 us (5%)
  between operations  0.66 us (1%)
    pallas_call x1, Pallas kernels, local(): pl.pallas_call(functools.partial(kernel, plan), out_shape=jax.ShapeDtypeS...  41.5 us
    unnamed x1, local copies, waits for them, and re-layouts  2.29 us

profile of v2, /device:TPU:1, one launch (start us, length us, event | category | flops | bytes accessed | tf_op | source)
XLA Modules:
  0.0 44.5 jit_solution(15371596543418756174)
XLA Ops:
  0.7 41.5 %routed_attention.1 = bf16[128,4096]{1,0:T(8,128)(2,1)} custom-call(s32[8]{0:T(128)} %refs_0_.1, s32[16]{0:T(128)} %refs_1_.1, s32[1]{0:T(128)S(6)} %copy.15.refs_2_, bf16[128,4096]{1,0:T(8,128)(2,1)} %refs_3_.1, bf16[8192,256]{1,0:T(8,128)(2,1)} %refs_4_.1, bf16[8192,128]{1,0:T(8,128)(2,1)} %refs_5_.1, bf16[256,8192]{1,0:T(8,128)(2,1)} %refs_6_.1, ...), custom_call_target="tpu_custom_call" | custom-call | tf_op jit(solution)/shard_map/routed_attention/pallas_call | solution.py:429
  42.2 2.3 %copy.16 = bf16[128,4096]{1,0:T(8,128)(2,1)} copy(bf16[128,4096]{1,0:T(8,128)(2,1)} %routed_attention.1) | data formatting | bytes 2097152

commit v3 on v2

--- a/solution.py
+++ b/solution.py
@@ -69,6 +69,12 @@
         load(4, r["rope"], r["rope_v"]),
     ]
     load_tokens, load_q, load_kv, load_wo, load_rope = loads
+    tables = [
+        pltpu.make_async_copy(r[name], r[name + "_s"], r["table_sem"].at[index])
+        for index, name in enumerate(("req", "pool"))
+    ]
+    for copy in tables:
+        copy.start()
     raw = [r[f"raw{index}"] for index in range(n)]
     give = [r[f"give{index}"] for index in range(n)]
     sends = [r[f"sends{index}"] for index in range(n)]
@@ -157,8 +163,11 @@
     pair_small = pair_copy(4, r["small_all"].at[side], r["small_all"].at[side])
     pair_shrink = pair_copy(5, r["shrink_own"], r["shrink_other"])
 
+    for copy in tables:
+        copy.wait()
+
     def facts(target):
-        wanted = r["pool"][r["req"][target]]
+        wanted = r["pool_s"][r["req_s"][target]]
         owner = lax.div(wanted, count)
         owner_level = lax.div(owner, 2)
         away = jnp.where(lax.rem(owner_level, 2) == lax.rem(level, 2), 0, 2)
@@ -408,6 +417,9 @@
         up_maps=pltpu.VMEM((3 * rank, 2 * q_here + 2 * kv_here), bf16),
         out_down=pltpu.VMEM((rank, 2 * q_here), bf16),
         attended=pltpu.VMEM((rows, 2 * q_here), bf16),
+        req_s=pltpu.SMEM(req.shape, jnp.int32),
+        pool_s=pltpu.SMEM(pool.shape, jnp.int32),
+        table_sem=pltpu.SemaphoreType.DMA((2,)),
         load_sem=pltpu.SemaphoreType.DMA((5 + 2 * len(pieces) + 6,)),
         hop_send=pltpu.SemaphoreType.DMA((3, len(pieces))),
         hop_recv=pltpu.SemaphoreType.DMA((3, len(pieces))),
@@ -417,26 +429,26 @@
         pair_send=pltpu.SemaphoreType.DMA((6,)),
         pair_recv=pltpu.SemaphoreType.DMA((6,)),
     )
-    operands = ["req", "pool", "lengths", "tokens", "qw", "kvw", "ow", "adm", "aqu", "akv", "aod", "aou", "rope"]
+    operands = ["lengths", "req", "pool", "tokens", "qw", "kvw", "ow", "adm", "aqu", "akv", "aod", "aou", "rope"]
     plan = dict(
         names=operands + ["out"] + list(scratch),
         levels=levels, count=count, rank=rank, width=width, q_here=q_here, kv_here=kv_here,
         pieces=pieces,
     )
     rope = jnp.asarray(rotary_tables(rows, HEAD_SIZE))
-    smem = pl.BlockSpec(memory_space=pltpu.SMEM)
+    arrays = (req, pool, tokens, qw, kvw, ow, adm, aqu, akv, aod, aou, rope)
     hbm = pl.BlockSpec(memory_space=pl.ANY)
     return pl.pallas_call(
         functools.partial(kernel, plan),
         out_shape=jax.ShapeDtypeStruct((rows, out_width), bf16),
-        in_specs=[smem] * 3 + [hbm] * 10,
+        in_specs=[pl.BlockSpec(memory_space=pltpu.SMEM)] + [hbm] * len(arrays),
         out_specs=pl.BlockSpec(memory_space=pltpu.VMEM),
         scratch_shapes=list(scratch.values()),
         compiler_params=pltpu.CompilerParams(
-            collective_id=0, has_side_effects=True, vmem_limit_bytes=60 * 1024 * 1024
+            collective_id=0, has_side_effects=True, vmem_limit_bytes=50 * 1024 * 1024
         ),
         name="routed_attention",
-    )(req, pool, lengths, tokens, qw, kvw, ow, adm, aqu, akv, aod, aou, rope)
+    )(lengths, *[pltpu.with_memory_space_constraint(array, pltpu.HBM) for array in arrays])
 
 
 def solution(mesh):

time: 44.6 us -> 42 us (0.942)
  local copies, waits for them, and re-layouts: 2.29 us -> 0.97 us
  Pallas kernels: 41.5 us -> 40.2 us
    pallas_call x1, Pallas kernels: 41.5 us -> 40.2 us  [local(): pl.pallas_call(functools.partial(kernel, plan), out_shape=jax.ShapeDtypeS...]
    unnamed x1, local copies, waits for them, and re-layouts: 2.29 us -> 0.97 us
where the time goes in v3:
time: 42 us; the launch traced here: 41.8 us
  Pallas kernels  40.2 us (96%)
  local copies, waits for them, and re-layouts  0.97 us (2%)
  between operations  0.66 us (2%)
    pallas_call x1, Pallas kernels, local(): pl.pallas_call(functools.partial(kernel, plan), out_shape=jax.ShapeDtypeS...  40.2 us
    unnamed x1, local copies, waits for them, and re-layouts  0.97 us

profile of v3, /device:TPU:1, one launch (start us, length us, event | category | flops | bytes accessed | tf_op | source)
XLA Modules:
  0.0 41.8 jit_solution(16657502206965055060)
XLA Ops:
  0.7 40.2 %routed_attention.1 = bf16[128,4096]{1,0:T(8,128)(2,1)S(1)} custom-call(s32[1]{0:T(128)S(6)} %copy.15.refs_0_, s32[8]{0:T(128)} %refs_1_.1, s32[16]{0:T(128)} %refs_2_.1, bf16[128,4096]{1,0:T(8,128)(2,1)} %refs_3_.1, bf16[8192,256]{1,0:T(8,128)(2,1)} %refs_4_.1, bf16[8192,128]{1,0:T(8,128)(2,1)} %refs_5_.1, bf16[256,8192]{1,0:T(8,128)(2,1)} %refs_6_.1, ...), custom_call_target="tpu_custom_call" | custom-call | tf_op jit(solution)/shard_map/routed_attention/pallas_call | solution.py:441
  40.9 1.0 %copy.16 = bf16[128,4096]{1,0:T(8,128)(2,1)} copy(bf16[128,4096]{1,0:T(8,128)(2,1)S(1)} %routed_attention.1) | data formatting | bytes 2097152

commit v4 on v3

--- a/solution.py
+++ b/solution.py
@@ -9,13 +9,15 @@
 from jax.sharding import PartitionSpec as P
 
 HEAD_SIZE = 128
-DOWN_PIECES = 8
-UP_PIECES = 2
+DOWN_PARTS = (2, 2, 2, 2, 2, 2, 2, 2)
+UP_PARTS = (6, 6, 4)
 BASE_PIECES = 8
-AHEAD = 2
+AHEAD_A = 2
+AHEAD_B = 1
 LAG_C = 1
 LAG_P = 3
-CHOOSE_1 = 9
+EARLY = 2
+TAIL = (2,)
 MESH = pl.DeviceIdType.MESH
 
 
@@ -95,7 +97,7 @@
             else:
                 src = r["adm" if family == "down" else "aou"]
                 span = spans[index]
-                at = pl.ds(pl.multiple_of((2 * number + half) * span, span), span)
+                at = pl.ds(pl.multiple_of(number + half * span, 128), span)
                 copies.append(load(len(loads) + 2 * index + slot, src.at[:, :, at], dst))
         piece_loads.append(copies)
     for copies in piece_loads:
@@ -109,19 +111,37 @@
     def greet(device):
         pl.semaphore_signal(barrier, inc=1, device_id=device, device_id_type=MESH)
 
-    greet(core_mate)
-    for other in range(2 * levels):
-        other_hub = other // 2 == hub_of(other // 4, levels)
-
-        @pl.when((me != other) if other_hub else ((me != other) & is_hub))
-        def _():
-            greet((group, other, side))
-
-    @pl.when(is_end)
+    for device in (core_mate, col_mate, level_mate):
+        greet(device)
+
+    def other_hubs(action):
+        for other in range(pairs):
+
+            @pl.when(is_hub & (pair != other))
+            def _():
+                action((group, 2 * hub_of(other, levels) + col, side))
+
+    other_hubs(greet)
+    pl.semaphore_wait(barrier, jnp.where(is_hub, pairs + 2, 3))
+
+    @pl.when(is_hub)
     def _():
-        greet(col_mate)
-
-    pl.semaphore_wait(barrier, jnp.where(is_hub, 2 * levels, 2 * pairs + 2))
+        pl.semaphore_signal(r["met"], inc=1, device_id=col_mate, device_id_type=MESH)
+
+    def meet():
+        @pl.when(is_hub)
+        def _():
+            pl.semaphore_wait(r["met"], 1)
+
+        other_hubs(
+            lambda device: pl.semaphore_signal(
+                r["met_hubs"], inc=1, device_id=device, device_id_type=MESH
+            )
+        )
+
+        @pl.when(is_hub)
+        def _():
+            pl.semaphore_wait(r["met_hubs"], pairs - 1)
 
     def remote(src, dst, send_sem, recv_sem, device):
         return pltpu.make_async_remote_copy(
@@ -183,11 +203,12 @@
     mul = lambda a, b: jnp.dot(a, b, preferred_element_type=jnp.float32)
     three = 3 * rank
 
-    def start(index):
+    def start_a(index):
         for copy in piece_loads[index]:
             copy.wait()
         copy_a(index).start()
 
+    def start_b(index):
         @pl.when(is_end)
         def _():
             copy_b_own(index).start()
@@ -227,20 +248,32 @@
         for half in range(2):
             value = hubs[index][half, mine[1]]
             if family == "down":
-                at = (2 * number + half) * spans[index]
+                at = number + half * spans[index]
                 x_part = r["x"][side, :, at : at + spans[index]]
                 r["shrink_own"][:, :three] += contract(x_part, value)
             elif family == "small":
                 r["small_all"][side, half] = value
             else:
-                r["up_all"][number, half] = value
+                at = number + half * spans[index]
+                r["up_all"][:, at : at + spans[index]] = value
         if family == "small":
             pair_small.start()
 
-    for index in range(AHEAD):
-        start(index)
+    done = {start_a: 0, start_b: 0, relay: 0, choose: 0, pick: 0}
+    lags = {start_a: -AHEAD_A, start_b: -AHEAD_B, relay: 0, choose: LAG_C, pick: LAG_C + LAG_P}
+
+    def up_to(action, index):
+        while done[action] <= min(index, n - 1):
+            action(done[action])
+            done[action] += 1
+
+    for index in range(AHEAD_A):
+        up_to(start_a, index)
+        if index < AHEAD_B:
+            up_to(start_b, index)
     for copy in (pair_tokens, pair_kv, pair_q, pair_wo):
         copy.start()
+    meet()
 
     r["qacc"][...] = jnp.zeros_like(r["qacc"])
     r["kvacc"][...] = jnp.zeros_like(r["kvacc"])
@@ -257,22 +290,15 @@
             r["kvacc"][...] += mul(x_block, r["wkv"][rows, :])
 
     last_down = max(i for i, p in enumerate(pieces) if p[0] == "down")
-    done = {start: AHEAD, relay: 0, choose: 0, pick: 0}
-    lags = {start: -AHEAD, relay: 0, choose: LAG_C, pick: LAG_C + LAG_P}
-
-    def up_to(action, index):
-        while done[action] <= min(index, n - 1):
-            action(done[action])
-            done[action] += 1
-
     base_done = 0
     steps = last_down + lags[pick] + 1
     first_base = steps - 5
     for number in range(steps):
-        for action in (start, relay, choose, pick):
+        for action in (start_a, start_b, relay, choose, pick):
             if action is pick and done[pick] == 0 and number == lags[pick]:
                 load_tokens.wait()
-            up_to(action, number - lags[action])
+            limit = last_down + EARLY if action is choose else n
+            up_to(action, min(number - lags[action], limit))
         if number == first_base:
             load_q.wait()
             load_kv.wait()
@@ -288,8 +314,13 @@
             base_done = upto
     pair_shrink.start()
 
-    up_to(relay, n)
-    up_to(choose, CHOOSE_1)
+    def tail_point(point):
+        up_to(relay, n)
+        for at in TAIL:
+            if at == point:
+                up_to(choose, done[choose])
+
+    tail_point(0)
     pair_small.wait_recv()
     lines = rank // 2
     for half in range(2):
@@ -306,6 +337,7 @@
     load_rope.wait()
     pair_wo.wait_recv()
     pair_shrink.wait_recv()
+    tail_point(1)
 
     shrink = (r["shrink_own"][:, :three] + r["shrink_other"][:, :three]).astype(jnp.bfloat16)
     added = mul(shrink, r["up_maps"][...])
@@ -318,7 +350,7 @@
 
     keys = rotate(kv[:, :HEAD_SIZE].astype(jnp.float32))
     values = kv[:, HEAD_SIZE:]
-    up_to(choose, n)
+    tail_point(2)
     heads = 2 * q_here // HEAD_SIZE
     length = r["lengths"][0]
     line = lax.broadcasted_iota(jnp.int32, (rows_here, rows_here), 0)
@@ -333,6 +365,8 @@
         expo = jnp.exp(scores - highest)
         weights = (expo / jnp.sum(expo, axis=1, keepdims=True)).astype(jnp.bfloat16)
         r["attended"][:, at] = mul(weights, values).astype(jnp.bfloat16)
+        tail_point(3 + head)
+    up_to(choose, n)
     low = contract(r["attended"][...], r["out_down"][...]).astype(jnp.bfloat16)
     tile = min(512, width)
 
@@ -346,14 +380,12 @@
         r["base"][:, cols] = base
 
     valid = lax.broadcasted_iota(jnp.int32, (rows_here, 1), 0) < length
-    span = r["up_all"].shape[-1]
-    for number in range(UP_PIECES):
-        up_to(pick, last_down + 1 + number)
-
+    for index in range(last_down + 1, n):
+        up_to(pick, index)
         for half in range(2):
-            at = (2 * number + half) * span
-            cols = slice(at, at + span)
-            total = r["base"][:, cols] + mul(low, r["up_all"][number, half])
+            at = pieces[index][1] + half * spans[index]
+            cols = slice(at, at + spans[index])
+            total = r["base"][:, cols] + mul(low, r["up_all"][:, cols])
             r["out"][:, cols] = jnp.where(valid, total, 0.0).astype(jnp.bfloat16)
 
     for index in range(n):
@@ -383,19 +415,17 @@
     q_here, kv_here = qw.shape[1], kvw.shape[1]
     levels = size // 2
     small_width = q_here + kv_here + q_here
-    down_span, up_span = width // (2 * DOWN_PIECES), out_width // (2 * UP_PIECES)
-    pieces = [("down", i) for i in range(DOWN_PIECES)]
-    pieces.insert(0, ("small", 0))
-    pieces += [("up", i) for i in range(UP_PIECES)]
-    shapes = {
-        "down": (adm.shape[1], down_span),
-        "small": (rank // 2, small_width),
-        "up": (rank, up_span),
-    }
+    pieces = [("small", 0, rank // 2, small_width)]
+    for family, lines, whole, parts in (
+        ("down", adm.shape[1], width, DOWN_PARTS),
+        ("up", rank, out_width, UP_PARTS),
+    ):
+        unit = whole // (2 * sum(parts))
+        for index, part in enumerate(parts):
+            pieces.append((family, 2 * unit * sum(parts[:index]), lines, unit * part))
     bf16, f32 = jnp.bfloat16, jnp.float32
     scratch = {}
-    for index, (family, _) in enumerate(pieces):
-        lines, span = shapes[family]
+    for index, (_, _, lines, span) in enumerate(pieces):
         kinds = {
             "raw": (4 * count,), "give": (count,), "sends": (size,),
             "hubs": (2, levels // 2),
@@ -404,7 +434,7 @@
             scratch[f"{kind}{index}"] = pltpu.VMEM((*lead, lines, span), bf16)
     scratch.update(
         small_all=pltpu.VMEM((2, 2, rank // 2, small_width), bf16),
-        up_all=pltpu.VMEM((UP_PIECES, 2, rank, up_span), bf16),
+        up_all=pltpu.VMEM((rank, out_width), bf16),
         x=pltpu.VMEM((2, rows, width), bf16),
         wq=pltpu.VMEM((qw.shape[0], 2 * q_here), bf16),
         wkv=pltpu.VMEM((kvw.shape[0], 2 * kv_here), bf16),
@@ -419,6 +449,8 @@
         attended=pltpu.VMEM((rows, 2 * q_here), bf16),
         req_s=pltpu.SMEM(req.shape, jnp.int32),
         pool_s=pltpu.SMEM(pool.shape, jnp.int32),
+        met=pltpu.SemaphoreType.REGULAR,
+        met_hubs=pltpu.SemaphoreType.REGULAR,
         table_sem=pltpu.SemaphoreType.DMA((2,)),
         load_sem=pltpu.SemaphoreType.DMA((5 + 2 * len(pieces) + 6,)),
         hop_send=pltpu.SemaphoreType.DMA((3, len(pieces))),
@@ -433,7 +465,7 @@
     plan = dict(
         names=operands + ["out"] + list(scratch),
         levels=levels, count=count, rank=rank, width=width, q_here=q_here, kv_here=kv_here,
-        pieces=pieces,
+        pieces=[piece[:2] for piece in pieces],
     )
     rope = jnp.asarray(rotary_tables(rows, HEAD_SIZE))
     arrays = (req, pool, tokens, qw, kvw, ow, adm, aqu, akv, aod, aou, rope)

time: 42 us -> 40.9 us (0.974)
  Pallas kernels: 40.2 us -> 39.1 us
    pallas_call x1, Pallas kernels: 40.2 us -> 39.1 us  [local(): pl.pallas_call(functools.partial(kernel, plan), out_shape=jax.ShapeDtypeS...]
where the time goes in v4:
time: 40.9 us; the launch traced here: 40.7 us
  Pallas kernels  39.1 us (96%)
  local copies, waits for them, and re-layouts  0.97 us (2%)
  between operations  0.66 us (2%)
    pallas_call x1, Pallas kernels, local(): pl.pallas_call(functools.partial(kernel, plan), out_shape=jax.ShapeDtypeS...  39.1 us
    unnamed x1, local copies, waits for them, and re-layouts  0.97 us

profile of v4, /device:TPU:1, one launch (start us, length us, event | category | flops | bytes accessed | tf_op | source)
XLA Modules:
  0.0 40.7 jit_solution(3526886447645459331)
XLA Ops:
  0.7 39.1 %routed_attention.1 = bf16[128,4096]{1,0:T(8,128)(2,1)S(1)} custom-call(s32[1]{0:T(128)S(6)} %copy.15.refs_0_, s32[8]{0:T(128)} %refs_1_.1, s32[16]{0:T(128)} %refs_2_.1, bf16[128,4096]{1,0:T(8,128)(2,1)} %refs_3_.1, bf16[8192,256]{1,0:T(8,128)(2,1)} %refs_4_.1, bf16[8192,128]{1,0:T(8,128)(2,1)} %refs_5_.1, bf16[256,8192]{1,0:T(8,128)(2,1)} %refs_6_.1, ...), custom_call_target="tpu_custom_call" | custom-call | tf_op jit(solution)/shard_map/routed_attention/pallas_call | solution.py:473
  39.8 1.0 %copy.16 = bf16[128,4096]{1,0:T(8,128)(2,1)} copy(bf16[128,4096]{1,0:T(8,128)(2,1)S(1)} %routed_attention.1) | data formatting | bytes 2097152

commit v5 on v4

--- a/solution.py
+++ b/solution.py
@@ -10,14 +10,15 @@
 
 HEAD_SIZE = 128
 DOWN_PARTS = (2, 2, 2, 2, 2, 2, 2, 2)
-UP_PARTS = (6, 6, 4)
+UP_PARTS = (8, 8)
 BASE_PIECES = 8
 AHEAD_A = 2
-AHEAD_B = 1
+AHEAD_B = 0
+FIRST_B = 2
 LAG_C = 1
 LAG_P = 3
 EARLY = 2
-TAIL = (2,)
+TAIL = ()
 MESH = pl.DeviceIdType.MESH
 
 
@@ -214,10 +215,9 @@
             copy_b_own(index).start()
 
     def relay(index):
-        copy_a(index).wait_recv()
-
         @pl.when(is_end)
         def _():
+            copy_a(index).wait_recv()
             copy_b_relay(index).start()
 
     send_order = sorted(range(2 * levels), key=lambda to: -abs(2 * (to // 2) + 1 - levels))
@@ -225,6 +225,7 @@
     def choose(index):
         @pl.when(is_hub)
         def _():
+            copy_a(index).wait_recv()
             copy_b_own(index).wait_recv()
             copy_b_relay(index).wait_recv()
             for to in send_order:
@@ -269,7 +270,7 @@
 
     for index in range(AHEAD_A):
         up_to(start_a, index)
-        if index < AHEAD_B:
+        if index < FIRST_B:
             up_to(start_b, index)
     for copy in (pair_tokens, pair_kv, pair_q, pair_wo):
         copy.start()

time: 40.9 us -> 39.5 us (0.966)
  Pallas kernels: 39.1 us -> 37.7 us
    pallas_call x1, Pallas kernels: 39.1 us -> 37.7 us  [local(): pl.pallas_call(functools.partial(kernel, plan), out_shape=jax.ShapeDtypeS...]
where the time goes in v5:
time: 39.5 us; the launch traced here: 39.3 us
  Pallas kernels  37.7 us (95%)
  local copies, waits for them, and re-layouts  0.97 us (2%)
  between operations  0.66 us (2%)
    pallas_call x1, Pallas kernels, local(): pl.pallas_call(functools.partial(kernel, plan), out_shape=jax.ShapeDtypeS...  37.7 us
    unnamed x1, local copies, waits for them, and re-layouts  0.97 us

profile of v5, /device:TPU:1, one launch (start us, length us, event | category | flops | bytes accessed | tf_op | source)
XLA Modules:
  0.0 39.3 jit_solution(8857767357242153727)
XLA Ops:
  0.7 37.7 %routed_attention.1 = bf16[128,4096]{1,0:T(8,128)(2,1)S(1)} custom-call(s32[1]{0:T(128)S(6)} %copy.15.refs_0_, s32[8]{0:T(128)} %refs_1_.1, s32[16]{0:T(128)} %refs_2_.1, bf16[128,4096]{1,0:T(8,128)(2,1)} %refs_3_.1, bf16[8192,256]{1,0:T(8,128)(2,1)} %refs_4_.1, bf16[8192,128]{1,0:T(8,128)(2,1)} %refs_5_.1, bf16[256,8192]{1,0:T(8,128)(2,1)} %refs_6_.1, ...), custom_call_target="tpu_custom_call" | custom-call | tf_op jit(solution)/shard_map/routed_attention/pallas_call | solution.py:474
  38.4 1.0 %copy.16 = bf16[128,4096]{1,0:T(8,128)(2,1)} copy(bf16[128,4096]{1,0:T(8,128)(2,1)S(1)} %routed_attention.1) | data formatting | bytes 2097152

commit v6 on v5

--- a/solution.py
+++ b/solution.py
@@ -57,6 +57,22 @@
     col_mate = (group, level * 2 + 1 - col, side)
     level_mate = (group, mate * 2 + col, side)
 
+    barrier = pltpu.get_barrier_semaphore()
+
+    def greet(device):
+        pl.semaphore_signal(barrier, inc=1, device_id=device, device_id_type=MESH)
+
+    for device in (core_mate, col_mate, level_mate):
+        greet(device)
+
+    def other_hubs(action):
+        for other in range(pairs):
+
+            @pl.when(is_hub & (pair != other))
+            def _():
+                action((group, 2 * hub_of(other, levels) + col, side))
+
+    other_hubs(greet)
     def load(index, src, dst):
         return pltpu.make_async_copy(src, dst, r["load_sem"].at[index])
 
@@ -107,22 +123,6 @@
     for copy in loads:
         copy.start()
 
-    barrier = pltpu.get_barrier_semaphore()
-
-    def greet(device):
-        pl.semaphore_signal(barrier, inc=1, device_id=device, device_id_type=MESH)
-
-    for device in (core_mate, col_mate, level_mate):
-        greet(device)
-
-    def other_hubs(action):
-        for other in range(pairs):
-
-            @pl.when(is_hub & (pair != other))
-            def _():
-                action((group, 2 * hub_of(other, levels) + col, side))
-
-    other_hubs(greet)
     pl.semaphore_wait(barrier, jnp.where(is_hub, pairs + 2, 3))
 
     @pl.when(is_hub)

time: 39.5 us -> 39.4 us (level)
  no operation moved by 1% of the time
where the time goes in v6:
time: 39.4 us; the launch traced here: 39.3 us
  Pallas kernels  37.6 us (95%)
  local copies, waits for them, and re-layouts  0.97 us (2%)
  between operations  0.66 us (2%)
    pallas_call x1, Pallas kernels, local(): pl.pallas_call(functools.partial(kernel, plan), out_shape=jax.ShapeDtypeS...  37.6 us
    unnamed x1, local copies, waits for them, and re-layouts  0.97 us

profile of v6, /device:TPU:1, one launch (start us, length us, event | category | flops | bytes accessed | tf_op | source)
XLA Modules:
  0.0 39.3 jit_solution(12956785926011524538)
XLA Ops:
  0.7 37.6 %routed_attention.1 = bf16[128,4096]{1,0:T(8,128)(2,1)S(1)} custom-call(s32[1]{0:T(128)S(6)} %copy.15.refs_0_, s32[8]{0:T(128)} %refs_1_.1, s32[16]{0:T(128)} %refs_2_.1, bf16[128,4096]{1,0:T(8,128)(2,1)} %refs_3_.1, bf16[8192,256]{1,0:T(8,128)(2,1)} %refs_4_.1, bf16[8192,128]{1,0:T(8,128)(2,1)} %refs_5_.1, bf16[256,8192]{1,0:T(8,128)(2,1)} %refs_6_.1, ...), custom_call_target="tpu_custom_call" | custom-call | tf_op jit(solution)/shard_map/routed_attention/pallas_call | solution.py:474
  38.3 1.0 %copy.16 = bf16[128,4096]{1,0:T(8,128)(2,1)} copy(bf16[128,4096]{1,0:T(8,128)(2,1)S(1)} %routed_attention.1) | data formatting | bytes 2097152
